TPU v7x, 128 devices: a whole 4x4x4 slice. The times are simulated.
128 devices in a mesh: head: 8 (over z, y_lo), pts: 16 (over y_hi, x, core).
Axes of the slice: x: 4, y: 4 (y_hi: 2, y_lo: 2; y = y_hi * 2 + y_lo), z: 4, core: 2. Of those that a mesh axis runs over, the one named last changes fastest.
Arguments:
- layer_inputs_trainorder: bfloat16 [786432, 256], P(('head', 'pts')), may hold values from -6 to 6
- inference_placement: int32 [786432], P(('head', 'pts')), may hold values from 0 to 786431, as said below
- initial_layernorm_gain: float32 [256], replicated, may hold values from 0.1 to 1.9
- initial_layernorm_offset: float32 [256], replicated, may hold values from -2 to 2
- attribute_projection: bfloat16 [256, 256], replicated, may hold values from -0.375 to 0.375
- assignment_feeder_projection: bfloat16 [256, 256], replicated, may hold values from -0.375 to 0.375
- partition_projection: bfloat16 [16, 32], replicated, may hold values from -1.5 to 1.5
- partition_offset: float32 [32], replicated, may hold values from -4 to 4
- softmax_sharpness: float32 [16], P('head'), may hold values from 0.03 to 1
- partition_question_map: float32 [16, 16], replicated, may hold values from -1.5 to 1.5
- partition_lookup_map: float32 [16, 16], replicated, may hold values from -1.5 to 1.5
- partition_content_map: float32 [16, 16], replicated, may hold values from -1.5 to 1.5
- emitted_projection: bfloat16 [256, 256], replicated, may hold values from -0.375 to 0.375
- emitted_offset: float32 [256], replicated, may hold values from -2 to 2
- latter_layernorm_gain: float32 [256], replicated, may hold values from 0.1 to 1.9
- latter_layernorm_offset: float32 [256], replicated, may hold values from -2 to 2
- perceptron_entry_map: bfloat16 [256, 1024], replicated, may hold values from -0.375 to 0.375
- perceptron_entry_offset: float32 [1024], replicated, may hold values from -2 to 2
- perceptron_exit_map: bfloat16 [1024, 256], replicated, may hold values from -0.1875 to 0.1875
- perceptron_exit_offset: float32 [256], replicated, may hold values from -2 to 2
Outputs:
- served: bfloat16 [16, 49152, 256], P('pts', 'head')
Inputs may be any that keep to these rules, and one draw needn't show every extreme that they name: inference_placement is a permutation of all points; of the 6144 points of each aligned block of the training order, exactly 48 go to each aligned block of 6144 serving positions.
All inputs are finite; a program needn't handle non-finite values.
Results may differ from a plain program's by a relative error of at most 0.0035.
The roundings to bfloat16 on the way count: a program that leaves them out, or rounds other values in their place, can miss the bound.
Values may be sent and summed in bfloat16 or wider, within the bound.
A program may use at most 128 MiB of HBM per device.

v0:
```python
import math
import jax
import jax.numpy as jnp
from jax import lax
from jax.sharding import Mesh
from jax.sharding import PartitionSpec as P

DH = 16
HEAD_PTS = ("head_0", "head_1", "pts_0", "pts_1", "pts_2")
HEAD = ("head_0", "head_1")
PTS = ("pts_0", "pts_1", "pts_2")


def from_everyone(array, axis):
    copies = jnp.broadcast_to(array, (lax.axis_size(axis), *array.shape))
    return lax.all_to_all(copies, axis, split_axis=0, concat_axis=0, tiled=True)


def in_order(tiles, dim):
    tiles = jnp.moveaxis(tiles, 0, dim)
    dims = tiles.shape
    return tiles.reshape(*dims[:dim], dims[dim] * dims[dim + 1], *dims[dim + 2 :])


def gather_directly(array, axis, dim):
    tiles = from_everyone(array, axis)
    return in_order(tiles, dim)


def one_axis_at_a_time(array, axes):
    for axis in axes:
        array = lax.psum(array, axis)
    return array


def layer_norm(row_block, gain_vec, bias_vec):
    row_mean = jnp.mean(row_block, axis=-1, keepdims=True)
    centred = row_block - row_mean
    spread = jnp.mean(centred * centred, axis=-1, keepdims=True)
    return centred * lax.rsqrt(spread + 1e-05) * gain_vec + bias_vec


def move_rows(rows, labels, ordering):
    arrived = lax.all_to_all(rows[ordering], HEAD_PTS, split_axis=0, concat_axis=0, tiled=True)
    arrived_labels = lax.all_to_all(labels, HEAD_PTS, split_axis=0, concat_axis=0, tiled=True)
    placed = jnp.argsort(arrived_labels[:, 0])
    return (arrived[placed], arrived_labels[placed, 1])


def slice_attention(
    totals, numerator, partition_question_map, partition_lookup_map, partition_content_map
):
    slice_token = numerator / (totals + 1e-05)[:, :, None]
    highest_mode = lax.Precision.HIGHEST
    query_rows = jnp.einsum(
        "izn,nu->izu", slice_token, partition_question_map, precision=highest_mode
    )
    key_vectors = jnp.einsum(
        "izn,nu->izu", slice_token, partition_lookup_map, precision=highest_mode
    )
    value_rows = jnp.einsum(
        "izn,nu->izu", slice_token, partition_content_map, precision=highest_mode
    )
    score_scale = 1.0 / math.sqrt(DH)
    scores = (
        jnp.einsum("hme,hne->hmn", query_rows, key_vectors, precision=highest_mode) * score_scale
    )
    attention = jax.nn.softmax(scores, axis=-1)
    return jnp.einsum("hmn,hne->hme", attention, value_rows, precision=highest_mode).astype(
        jnp.bfloat16
    )


def finish_rows(
    residual_rows,
    blended_rows,
    emitted_projection,
    emitted_offset,
    latter_layernorm_gain,
    latter_layernorm_offset,
    perceptron_entry_map,
    perceptron_entry_offset,
    perceptron_exit_map,
    perceptron_exit_offset,
):
    hidden = (
        residual_rows.astype(jnp.float32)
        + jnp.dot(blended_rows, emitted_projection, preferred_element_type=jnp.float32)
        + emitted_offset
    )
    normed_two = layer_norm(hidden, latter_layernorm_gain, latter_layernorm_offset).astype(
        jnp.bfloat16
    )
    inner_act = jax.nn.gelu(
        jnp.dot(normed_two, perceptron_entry_map, preferred_element_type=jnp.float32)
        + perceptron_entry_offset,
        approximate=False,
    ).astype(jnp.bfloat16)
    return (
        hidden
        + jnp.dot(inner_act, perceptron_exit_map, preferred_element_type=jnp.float32)
        + perceptron_exit_offset
    ).astype(jnp.bfloat16)


def body(
    layer_inputs_trainorder,
    inference_placement,
    initial_layernorm_gain,
    initial_layernorm_offset,
    attribute_projection,
    assignment_feeder_projection,
    partition_projection,
    partition_offset,
    softmax_sharpness,
    partition_question_map,
    partition_lookup_map,
    partition_content_map,
    emitted_projection,
    emitted_offset,
    latter_layernorm_gain,
    latter_layernorm_offset,
    perceptron_entry_map,
    perceptron_entry_offset,
    perceptron_exit_map,
    perceptron_exit_offset,
):
    groups = lax.axis_size(HEAD)
    shards = lax.axis_size(PTS)
    local_rows = layer_inputs_trainorder.shape[0]
    model_width = layer_inputs_trainorder.shape[1]
    dest_block = inference_placement // local_rows
    target = dest_block % groups * shards + dest_block // groups
    ordering = jnp.argsort(target, stable=True)
    anchor = lax.axis_index(HEAD_PTS) * local_rows + jnp.arange(local_rows, dtype=jnp.int32)
    labels = jnp.stack([inference_placement[ordering], anchor[ordering]], axis=1)
    sharpness_sequence = gather_directly(softmax_sharpness, HEAD, 0)
    every_attender = sharpness_sequence.shape[0]
    standardized_entries = layer_norm(
        layer_inputs_trainorder.astype(jnp.float32),
        initial_layernorm_gain,
        initial_layernorm_offset,
    ).astype(jnp.bfloat16)
    slice_feature_rows = (
        jnp.dot(standardized_entries, attribute_projection, preferred_element_type=jnp.float32)
        .astype(jnp.bfloat16)
        .reshape(local_rows, every_attender, DH)
    )
    middle = (
        jnp.dot(
            standardized_entries, assignment_feeder_projection, preferred_element_type=jnp.float32
        )
        .astype(jnp.bfloat16)
        .reshape(local_rows, every_attender, DH)
    )
    partition_scores_raw = jnp.einsum(
        "rhd,dm->rhm", middle, partition_projection, preferred_element_type=jnp.float32
    )
    partition_scores_raw = (partition_scores_raw + partition_offset) / sharpness_sequence[:, None]
    coefficient_array = jax.nn.softmax(partition_scores_raw, axis=-1)
    coefficients_halfprecision = coefficient_array.astype(jnp.bfloat16)
    totals = jnp.sum(coefficient_array, axis=0)
    numerator = jnp.einsum(
        "qct,qcv->ctv",
        coefficients_halfprecision,
        slice_feature_rows,
        preferred_element_type=jnp.float32,
    )
    totals, numerator = (
        one_axis_at_a_time(totals, HEAD_PTS),
        one_axis_at_a_time(numerator, HEAD_PTS),
    )
    slice_output = slice_attention(
        totals, numerator, partition_question_map, partition_lookup_map, partition_content_map
    )
    blended_rows = (
        jnp.einsum(
            "fny,nyp->fnp",
            coefficients_halfprecision,
            slice_output,
            preferred_element_type=jnp.float32,
        )
        .astype(jnp.bfloat16)
        .reshape(local_rows, model_width)
    )
    result = finish_rows(
        layer_inputs_trainorder,
        blended_rows,
        emitted_projection,
        emitted_offset,
        latter_layernorm_gain,
        latter_layernorm_offset,
        perceptron_entry_map,
        perceptron_entry_offset,
        perceptron_exit_map,
        perceptron_exit_offset,
    )
    served, unused = move_rows(result, labels, ordering)
    return served[None]


def solution(mesh):
    torus = Mesh(
        mesh.devices.reshape(4, 2, 2, 4, 2), ("head_0", "head_1", "pts_0", "pts_1", "pts_2")
    )
    in_specs = (
        P(HEAD_PTS, None),
        P(HEAD_PTS),
        P(),
        P(),
        P(),
        P(),
        P(),
        P(),
        P(HEAD),
        P(),
        P(),
        P(),
        P(),
        P(),
        P(),
        P(),
        P(),
        P(),
        P(),
        P(),
    )
    out_specs = P(PTS, HEAD, None)
    return jax.shard_map(body, mesh=torus, in_specs=in_specs, out_specs=out_specs, check_vma=False)
```

profile of v0, /device:TPU:1, one launch (start us, length us, event | category | flops | bytes accessed | tf_op | source)
XLA Modules:
  0.0 388.4 jit_solution(6724094378203701550)
XLA Ops:
  0.0 0.0 copy-start
  0.0 0.0 copy-start.12
  0.0 1.3 broadcast_in_dim.8
  1.3 6.9 %all-to-all-start = ((f32[8,1,2]{2,1,0:T(1,128)}), f32[8,1,2]{2,1,0:T(1,128)S(1)}, u32[]{:S(2)}, u32[]{:S(2)}) async-start(f32[8,1,2]{2,1,0:T(1,128)} %broadcast_in_dim.8), calls=%async_computation | async-start | bytes 8192 | tf_op jit(solution)/shard_map/all_to_all | solution.py:16
  8.2 4.6 %copy.45 = bf16[6144,256]{0,1:T(8,128)(2,1)} copy(bf16[6144,256]{1,0:T(8,128)(2,1)} %param.20) | data formatting | bytes 6291456 | tf_op args[0]
  12.8 2.6 convert_reduce_fusion
  15.4 2.7 fusion.27
  18.2 0.0 copy-start.2
  18.2 5.3 %convolution_convert_fusion.2 = bf16[6144,256]{0,1:T(8,128)(2,1)} fusion(bf16[256,256]{1,0:T(8,128)(2,1)S(1)} %copy-done.12, bf16[6144,256]{0,1:T(8,128)(2,1)} %copy.45, f32[256]{0:T(256)S(1)} %copy-done.19, f32[256]{0:T(256)S(1)} %copy-done.20, f32[6144]{0:T(1024)S(1)} %add_rsqrt_fusion.1, f32[6144]{0:T(1024)S(1)} %broadcast_multiply_fusion.1), kind=kOutput, calls=%fused_computation.36 | convolution fusion | flops 816316416 | bytes 6473728 | tf_op jit(solution)/shard_map/dot_general | solution.py:150
  23.5 3.4 convolution_convert_fusion.1
  27.0 6.7 %sort.34 = (s32[6144]{0:T(1024)}, s32[6144]{0:T(1024)S(1)}) sort(s32[6144]{0:T(1024)S(1)} %fusion.46, s32[6144]{0:T(1024)S(1)} %iota.11), dimensions={0}, to_apply=%region_19.20 | sort | flops 79872 | bytes 98304 | tf_op jit(solution)/shard_map/jit(argsort)/sort | solution.py:134
  33.7 0.0 copy-start.7
  33.7 34.3 %gather_fusion.1 = s32[6144]{0:T(1024)S(1)} fusion(s32[6144]{0:T(1024)S(1)} %copy-done.2, s32[6144]{0:T(1024)S(1)} %get-tuple-element.27), kind=kCustom, calls=%fused_computation.1 | custom fusion | bytes 73728 | tf_op jit(solution)/shard_map/gather | solution.py:136
  68.0 0.0 copy-done.7
  68.1 0.0 copy-start.17
  68.1 0.0 copy-start.24
  68.1 34.3 %gather_fusion.2 = s32[6144]{0:T(1024)S(1)} fusion(s32[6144]{0:T(1024)S(1)} %get-tuple-element.28, s32[6144]{0:T(1024)S(1)} %get-tuple-element.27), kind=kCustom, calls=%fused_computation.2 | custom fusion | bytes 73728 | tf_op jit(solution)/shard_map/gather | solution.py:136
  102.4 0.1 stack.10
  102.5 0.1 stack.9
  102.6 0.8 copy.52
  103.3 0.0 all-to-all-done
  103.3 11.3 %all-to-all-start.2 = ((s32[128,48,2]{1,2,0:T(2,128)}), s32[128,48,2]{1,2,0:T(2,128)}, u32[]{:S(2)}, u32[]{:S(2)}) async-start(s32[128,48,2]{1,2,0:T(2,128)} %copy.52), calls=%async_computation.2 | async-start | bytes 262144 | tf_op jit(solution)/shard_map/all_to_all | solution.py:45
  114.6 0.5 broadcast.103
  115.1 0.6 reduce.3
  115.8 0.1 div.64
  115.9 10.9 %fusion.93 = (f32[6144,16]{0,1:T(8,128)S(1)}, f32[6144,16,32]{0,2,1:T(8,128)}) fusion(bf16[6144,16,16]{0,2,1:T(8,128)(2,1)} %bitcast.48, f32[16]{0:T(128)S(1)} %div.64, f32[32]{0:T(128)S(1)} %copy-done.24, bf16[16,32]{1,0:T(8,128)(2,1)S(1)} %copy-done.17), kind=kOutput, calls=%fused_computation.125 | convolution fusion | flops 113246240 | bytes 16123072 | tf_op jit(solution)/shard_map/sub | solution.py:160
  126.8 9.1 %fusion.31 = (f32[16,32]{1,0:T(8,128)S(1)}, bf16[6144,16,32]{0,2,1:T(8,128)(2,1)}) fusion(f32[6144,16,32]{0,2,1:T(8,128)} %get-tuple-element.22, f32[6144,16]{0,1:T(8,128)S(1)} %get-tuple-element.21), kind=kLoop, calls=%fused_computation.47 | loop fusion | flops 9436672 | bytes 19269632 | tf_op jit(solution)/shard_map/reduce_sum | solution.py:162
  135.8 0.0 copy-done.6
  135.8 4.6 %fusion.98 = f32[16,32,16]{1,2,0:T(8,128)S(1)} fusion(bf16[6144,16,32]{0,2,1:T(8,128)(2,1)} %get-tuple-element.20, bf16[6144,16,16]{0,2,1:T(8,128)(2,1)S(1)} %bitcast.46), kind=kOutput, calls=%fused_computation.128 | convolution fusion | flops 100663296 | bytes 9469952 | tf_op jit(solution)/shard_map/qct,qcv->ctv/dot_general | solution.py:163
  140.4 15.4 %all-reduce.1 = (f32[16,32,16]{1,2,0:T(8,128)S(1)}, f32[16,32]{1,0:T(8,128)S(1)}) all-reduce(f32[16,32,16]{1,2,0:T(8,128)S(1)} %fusion.98, f32[16,32]{1,0:T(8,128)S(1)} %get-tuple-element.19), channel_id=1, replica_groups=mesh['head_0'=4,'head_1'=2,'pts_0'=2,'pts_1'=4,'pts_2'=2] {'head_0'}, use_global_device_ids=true, to_apply=%region_4.5 | all-reduce | flops 8704 | bytes 69632 | tf_op jit(solution)/shard_map/psum | solution.py:32
  155.8 7.7 %all-reduce.4 = (f32[16,32,16]{1,2,0:T(8,128)S(1)}, f32[16,32]{1,0:T(8,128)S(1)}) all-reduce(f32[16,32,16]{1,2,0:T(8,128)S(1)} %get-tuple-element.11, f32[16,32]{1,0:T(8,128)S(1)} %get-tuple-element.12), channel_id=1, replica_groups=mesh['head_0'=4,'head_1'=2,'pts_0'=2,'pts_1'=4,'pts_2'=2] {'head_1'}, use_global_device_ids=true, to_apply=%region_5.6 | all-reduce | flops 8704 | bytes 69632 | tf_op jit(solution)/shard_map/psum | solution.py:32
  163.5 10.4 %all-reduce.3 = (f32[16,32,16]{1,2,0:T(8,128)S(1)}, f32[16,32]{1,0:T(8,128)S(1)}) all-reduce(f32[16,32,16]{1,2,0:T(8,128)S(1)} %get-tuple-element.17, f32[16,32]{1,0:T(8,128)S(1)} %get-tuple-element.18), channel_id=1, replica_groups=mesh['head_0'=4,'head_1'=2,'pts_0'=2,'pts_1'=4,'pts_2'=2] {'pts_0'}, use_global_device_ids=true, to_apply=%region_6.7 | all-reduce | flops 8704 | bytes 69632 | tf_op jit(solution)/shard_map/psum | solution.py:32
  174.0 15.1 %all-reduce = (f32[16,32,16]{1,2,0:T(8,128)S(1)}, f32[16,32]{1,0:T(8,128)S(1)}) all-reduce(f32[16,32,16]{1,2,0:T(8,128)S(1)} %get-tuple-element.15, f32[16,32]{1,0:T(8,128)S(1)} %get-tuple-element.16), channel_id=1, replica_groups=mesh['head_0'=4,'head_1'=2,'pts_0'=2,'pts_1'=4,'pts_2'=2] {'pts_1'}, use_global_device_ids=true, to_apply=%region_7.8 | all-reduce | flops 8704 | bytes 69632 | tf_op jit(solution)/shard_map/psum | solution.py:32
  189.1 15.1 %all-reduce.2 = (f32[16,32,16]{1,2,0:T(8,128)S(1)}, f32[16,32]{1,0:T(8,128)S(1)}) all-reduce(f32[16,32,16]{1,2,0:T(8,128)S(1)} %get-tuple-element.9, f32[16,32]{1,0:T(8,128)S(1)} %get-tuple-element.10), channel_id=1, replica_groups=mesh['head_0'=4,'head_1'=2,'pts_0'=2,'pts_1'=4,'pts_2'=2] {'pts_2'}, use_global_device_ids=true, to_apply=%region_8.9 | all-reduce | flops 8704 | bytes 69632 | tf_op jit(solution)/shard_map/psum | solution.py:32
  204.1 0.0 copy-start.4
  204.1 0.0 copy-done.14
  204.2 0.3 fusion.56
  204.5 0.0 copy-done.15
  204.5 0.3 fusion.58
  204.8 0.3 fusion.54
  205.1 0.6 fusion.94
  205.8 0.1 fusion.42
  205.8 0.4 convolution_convert_fusion.3
  206.2 3.7 convolution_convert_fusion
  210.0 0.0 copy-start.18
  210.0 0.0 copy-start.21
  210.0 0.0 copy-start.22
  210.0 0.0 copy-done.9
  210.1 1.4 fusion.95
  211.5 0.7 multiply_reduce_fusion
  212.2 1.9 copy-done.5
  214.1 0.0 copy-start.11
  214.1 0.0 copy-start.23
  214.1 58.5 %fusion.119 = bf16[6144,1024]{1,0:T(8,128)(2,1)} fusion(f32[1024]{0:T(1024)S(1)} %copy-done.18, bf16[256,1024]{1,0:T(8,128)(2,1)S(1)} %copy-done, f32[6144,256]{0,1:T(8,128)S(1)} %get-tuple-element.26, f32[256]{0:T(256)S(1)} %copy-done.21, f32[256]{0:T(256)S(1)} %copy-done.22, f32[6144]{0:T(1024)S(1)} %add_rsqrt_fusion, ...), kind=kOutput, calls=%fused_computation.8.clone.clone.clone.clone.clone.clone.clone.clone.1 | convolution fusion | flops 3644325888 | bytes 19453952 | tf_op jit(solution)/shard_map/dot_general | solution.py:95
  272.6 15.5 %fusion.22 = bf16[6144,256]{0,1:T(8,128)(2,1)} fusion(f32[6144,256]{0,1:T(8,128)} %copy-done.5, bf16[1024,256]{1,0:T(8,128)(2,1)S(1)} %copy-done.11, f32[256]{0:T(256)S(1)} %copy-done.23, bf16[6144,1024]{1,0:T(8,128)(2,1)} %fusion.119), kind=kOutput, calls=%fused_computation.37 | convolution fusion | flops 3225944064 | bytes 22545408 | tf_op jit(solution)/shard_map/dot_general | solution.py:101
  288.1 3.2 copy.51
  291.3 25.1 %gather_fusion = bf16[6144,256]{1,0:T(8,128)(2,1)} fusion(bf16[6144,256]{1,0:T(8,128)(2,1)S(1)} %copy.51, s32[6144]{0:T(1024)S(1)} %copy-done.8), kind=kCustom, calls=%fused_computation | custom fusion | bytes 6316032 | tf_op jit(solution)/shard_map/gather | solution.py:44
  316.4 0.0 all-to-all-done.2
  316.4 4.7 %all-to-all-start.1 = ((bf16[128,48,256]{2,1,0:T(8,128)(2,1)}), bf16[128,48,256]{2,1,0:T(8,128)(2,1)}, u32[]{:S(2)}, u32[]{:S(2)}) async-start(bf16[128,48,256]{2,1,0:T(8,128)(2,1)} %bitcast.45), calls=%async_computation.1 | async-start | bytes 6291456 | tf_op jit(solution)/shard_map/all_to_all | solution.py:44
  321.1 0.9 copy.53
  322.0 0.1 all_to_all.23
  322.2 6.7 %sort.35 = (s32[6144]{0:T(1024)}, s32[6144]{0:T(1024)S(1)}) sort(s32[6144]{0:T(1024)S(1)} %bitcast.47, s32[6144]{0:T(1024)S(1)} %iota.13), dimensions={0}, to_apply=%region_20.21 | sort | flops 79872 | bytes 98304 | tf_op jit(solution)/shard_map/jit(argsort)/sort | solution.py:46
  328.9 33.4 %all-to-all-done.1 = bf16[128,48,256]{2,1,0:T(8,128)(2,1)} async-done(((bf16[128,48,256]{2,1,0:T(8,128)(2,1)}), bf16[128,48,256]{2,1,0:T(8,128)(2,1)}, u32[]{:S(2)}, u32[]{:S(2)}) %all-to-all-start.1) | async-done | bytes 3145760 | tf_op jit(solution)/shard_map/all_to_all | solution.py:44
  362.3 25.9 %gather_fusion.3 = bf16[6144,256]{1,0:T(8,128)(2,1)} fusion(bf16[6144,256]{1,0:T(8,128)(2,1)} %bitcast.9, s32[6144]{0:T(1024)S(1)} %fusion.48), kind=kCustom, calls=%fused_computation.3 | custom fusion | bytes 6316032 | tf_op jit(solution)/shard_map/gather | solution.py:47
  (44 shorter events, 0.2 us)
Async XLA Ops:
  0.0 214.1 %copy-start = (bf16[256,1024]{1,0:T(8,128)(2,1)S(1)}, bf16[256,1024]{1,0:T(8,128)(2,1)}, u32[]{:S(2)}) copy-start(bf16[256,1024]{1,0:T(8,128)(2,1)} %param.36) | copy-start | bytes 1572868
  0.0 18.2 %copy-start.20 = (f32[256]{0:T(256)S(1)}, f32[256]{0:T(256)}, u32[]{:S(2)}) copy-start(f32[256]{0:T(256)} %param.22) | copy-start | bytes 3076
  0.0 18.2 %copy-start.19 = (f32[256]{0:T(256)S(1)}, f32[256]{0:T(256)}, u32[]{:S(2)}) copy-start(f32[256]{0:T(256)} %param.23) | copy-start | bytes 3076
  0.0 18.2 %copy-start.12 = (bf16[256,256]{1,0:T(8,128)(2,1)S(1)}, bf16[256,256]{1,0:T(8,128)(2,1)}, u32[]{:S(2)}) copy-start(bf16[256,256]{1,0:T(8,128)(2,1)} %param.25) | copy-start | bytes 393220
  1.3 102.0 %all-to-all-start = ((f32[8,1,2]{2,1,0:T(1,128)}), f32[8,1,2]{2,1,0:T(1,128)S(1)}, u32[]{:S(2)}, u32[]{:S(2)}) async-start(f32[8,1,2]{2,1,0:T(1,128)} %broadcast_in_dim.8), calls=%async_computation | async-start | bytes 8192 | tf_op jit(solution)/shard_map/all_to_all | solution.py:16
  12.8 10.7 %copy-start.3 = (bf16[6144,256]{0,1:T(8,128)(2,1)S(1)}, bf16[6144,256]{0,1:T(8,128)(2,1)}, u32[]{:S(2)}) copy-start(bf16[6144,256]{0,1:T(8,128)(2,1)} %copy.45) | copy-start | bytes 9437188
  12.8 10.7 %copy-start.13 = (bf16[256,256]{1,0:T(8,128)(2,1)S(1)}, bf16[256,256]{1,0:T(8,128)(2,1)}, u32[]{:S(2)}) copy-start(bf16[256,256]{1,0:T(8,128)(2,1)} %param.24) | copy-start | bytes 393220
  18.2 8.7 %copy-start.2 = (s32[6144]{0:T(1024)S(1)}, s32[6144]{0:T(1024)}, u32[]{:S(2)}) copy-start(s32[6144]{0:T(1024)} %param.21) | copy-start | bytes 73732
  33.7 34.3 %copy-start.7 = (s32[6144]{0:T(1024)}, s32[6144]{0:T(1024)S(1)}, u32[]{:S(2)}) copy-start(s32[6144]{0:T(1024)S(1)} %get-tuple-element.27) | copy-start | bytes 73732
  68.1 47.8 %copy-start.17 = (bf16[16,32]{1,0:T(8,128)(2,1)S(1)}, bf16[16,32]{1,0:T(8,128)(2,1)}, u32[]{:S(2)}) copy-start(bf16[16,32]{1,0:T(8,128)(2,1)} %param.26) | copy-start | bytes 3076
  68.1 47.8 %copy-start.24 = (f32[32]{0:T(128)S(1)}, f32[32]{0:T(128)}, u32[]{:S(2)}) copy-start(f32[32]{0:T(128)} %param.27) | copy-start | bytes 388
  103.3 213.1 %all-to-all-start.2 = ((s32[128,48,2]{1,2,0:T(2,128)}), s32[128,48,2]{1,2,0:T(2,128)}, u32[]{:S(2)}, u32[]{:S(2)}) async-start(s32[128,48,2]{1,2,0:T(2,128)} %copy.52), calls=%async_computation.2 | async-start | bytes 262144 | tf_op jit(solution)/shard_map/all_to_all | solution.py:45
  126.8 9.1 %copy-start.6 = (bf16[6144,256]{0,1:T(8,128)(2,1)S(1)}, bf16[6144,256]{0,1:T(8,128)(2,1)}, u32[]{:S(2)}) copy-start(bf16[6144,256]{0,1:T(8,128)(2,1)} %convolution_convert_fusion.1) | copy-start | bytes 9437188
  126.8 77.4 %copy-start.14 = (f32[16,16]{1,0:T(8,128)S(1)}, f32[16,16]{1,0:T(8,128)}, u32[]{:S(2)}) copy-start(f32[16,16]{1,0:T(8,128)} %param.30) | copy-start | bytes 3076
  126.8 77.7 %copy-start.15 = (f32[16,16]{1,0:T(8,128)S(1)}, f32[16,16]{1,0:T(8,128)}, u32[]{:S(2)}) copy-start(f32[16,16]{1,0:T(8,128)} %param.29) | copy-start | bytes 3076
  126.8 78.0 %copy-start.16 = (f32[16,16]{1,0:T(8,128)S(1)}, f32[16,16]{1,0:T(8,128)}, u32[]{:S(2)}) copy-start(f32[16,16]{1,0:T(8,128)} %param.31) | copy-start | bytes 3076
  135.8 74.2 %copy-start.9 = (bf16[256,256]{1,0:T(8,128)(2,1)S(1)}, bf16[256,256]{1,0:T(8,128)(2,1)}, u32[]{:S(2)}) copy-start(bf16[256,256]{1,0:T(8,128)(2,1)} %param.32) | copy-start | bytes 393220
  135.8 74.2 %copy-start.10 = (f32[256]{0:T(256)S(1)}, f32[256]{0:T(256)}, u32[]{:S(2)}) copy-start(f32[256]{0:T(256)} %param.33) | copy-start | bytes 3076
  204.1 5.9 %copy-start.4 = (bf16[6144,256]{0,1:T(8,128)(2,1)S(1)}, bf16[6144,256]{0,1:T(8,128)(2,1)}, u32[]{:S(2)}) copy-start(bf16[6144,256]{0,1:T(8,128)(2,1)} %copy.45) | copy-start | bytes 9437188
  210.0 4.1 %copy-start.18 = (f32[1024]{0:T(1024)S(1)}, f32[1024]{0:T(1024)}, u32[]{:S(2)}) copy-start(f32[1024]{0:T(1024)} %param.37) | copy-start | bytes 12292
  210.0 4.1 %copy-start.21 = (f32[256]{0:T(256)S(1)}, f32[256]{0:T(256)}, u32[]{:S(2)}) copy-start(f32[256]{0:T(256)} %param.35) | copy-start | bytes 3076
  210.0 4.1 %copy-start.22 = (f32[256]{0:T(256)S(1)}, f32[256]{0:T(256)}, u32[]{:S(2)}) copy-start(f32[256]{0:T(256)} %param.34) | copy-start | bytes 3076
  211.5 2.6 copy-start.5
  214.1 58.5 %copy-start.11 = (bf16[1024,256]{1,0:T(8,128)(2,1)S(1)}, bf16[1024,256]{1,0:T(8,128)(2,1)}, u32[]{:S(2)}) copy-start(bf16[1024,256]{1,0:T(8,128)(2,1)} %param.38) | copy-start | bytes 1572868
  214.1 58.5 %copy-start.23 = (f32[256]{0:T(256)S(1)}, f32[256]{0:T(256)}, u32[]{:S(2)}) copy-start(f32[256]{0:T(256)} %param.39) | copy-start | bytes 3076
  272.6 18.7 %copy-start.8 = (s32[6144]{0:T(1024)S(1)}, s32[6144]{0:T(1024)}, u32[]{:S(2)}) copy-start(s32[6144]{0:T(1024)} %copy-done.7) | copy-start | bytes 73732
  316.4 45.9 %all-to-all-start.1 = ((bf16[128,48,256]{2,1,0:T(8,128)(2,1)}), bf16[128,48,256]{2,1,0:T(8,128)(2,1)}, u32[]{:S(2)}, u32[]{:S(2)}) async-start(bf16[128,48,256]{2,1,0:T(8,128)(2,1)} %bitcast.45), calls=%async_computation.1 | async-start | bytes 6291456 | tf_op jit(solution)/shard_map/all_to_all | solution.py:44
  362.3 25.9 %copy-start.1 = (bf16[256,1024]{1,0:T(8,128)(2,1)S(1)}, bf16[256,1024]{1,0:T(8,128)(2,1)}, u32[]{:S(2)}) copy-start(bf16[256,1024]{1,0:T(8,128)(2,1)} %param.36) | copy-start | bytes 1572868
where the time goes:
time: 396 us; the launch traced here: 388 us
  local copies, waits for them, and re-layouts  133 us (34%)
  matrix products  105 us (27%)
  blocking collectives  63.7 us (16%)
  waiting for transfers between devices  33.4 us (8%)
  other arithmetic  29.4 us (7%)
  starting transfers between devices  22.8 us (6%)
    psum x5, blocking collectives, one_axis_at_a_time(): array = lax.psum(array, axis)  63.7 us
    dot_general x1, matrix products, finish_rows(): jnp.dot(normed_two, perceptron_entry_map, preferred_element_type=jnp.floa...  58.5 us
    gather x1, local copies, waits for them, and re-layouts, body(): inference_placement[ordering]  34.3 us
    gather x1, local copies, waits for them, and re-layouts, body(): anchor[ordering]  34.3 us
    all_to_all x1, waiting for transfers between devices, move_rows(): lax.all_to_all(rows[ordering], HEAD_PTS, split_axis=0, concat_axis=0, til...  33.4 us
    gather x1, local copies, waits for them, and re-layouts, move_rows(): return (arrived[placed], arrived_labels[placed, 1])  25.9 us
    gather x1, local copies, waits for them, and re-layouts, move_rows(): rows[ordering]  25.1 us
    dot_general x1, matrix products, finish_rows(): jnp.dot(inner_act, perceptron_exit_map, preferred_element_type=jnp.float32)  15.5 us
  transfers between devices with their start and end apart: 3, of which 1 were waited for; matrix products, arithmetic and copies ran while one was open for 61% of the time, Pallas kernels for 0%

commit v1 on v0

--- a/solution.py
+++ b/solution.py
@@ -4,6 +4,7 @@
 from jax import lax
 from jax.sharding import Mesh
 from jax.sharding import PartitionSpec as P
+from jax.lax import all_gather
 
 DH = 16
 HEAD_PTS = ("head_0", "head_1", "pts_0", "pts_1", "pts_2")
@@ -29,7 +30,7 @@
 
 def one_axis_at_a_time(array, axes):
     for axis in axes:
-        array = lax.psum(array, axis)
+        array = all_gather(array, axis_name=axis).sum(axis=0)
     return array
 
 

time: 396 us -> 415 us (1.048)
  blocking collectives: 63.7 us -> 77.8 us
  starting transfers between devices: 22.8 us -> 27.8 us
    all_gather x0 -> x10, blocking collectives: none -> 77.8 us  [one_axis_at_a_time(): array = all_gather(array, axis_name=axis).sum(axis=0)]
    psum x5 -> x0, blocking collectives: 63.7 us -> none  [one_axis_at_a_time(): array = lax.psum(array, axis)]
    all_to_all x1, starting transfers between devices: 4.69 us -> 9.62 us  [move_rows(): lax.all_to_all(rows[ordering], HEAD_PTS, split_axis=0, concat_axis=0, til...]
  transfers between devices with their start and end apart: 3 -> 3, of which waited for: 1 -> 1; matrix products, arithmetic and copies ran while one was open for 61% -> 59% of each run, Pallas kernels for 0% -> 0%
where the time goes in v1:
time: 415 us; the launch traced here: 408 us
  local copies, waits for them, and re-layouts  133 us (32%)
  matrix products  105 us (25%)
  blocking collectives  77.8 us (19%)
  waiting for transfers between devices  33.3 us (8%)
  other arithmetic  29.5 us (7%)
  starting transfers between devices  27.8 us (7%)
    all_gather x10, blocking collectives, one_axis_at_a_time(): array = all_gather(array, axis_name=axis).sum(axis=0)  77.8 us
    dot_general x1, matrix products, finish_rows(): jnp.dot(normed_two, perceptron_entry_map, preferred_element_type=jnp.floa...  58.5 us
    gather x1, local copies, waits for them, and re-layouts, body(): inference_placement[ordering]  34.3 us
    gather x1, local copies, waits for them, and re-layouts, body(): anchor[ordering]  34.3 us
    all_to_all x1, waiting for transfers between devices, move_rows(): lax.all_to_all(rows[ordering], HEAD_PTS, split_axis=0, concat_axis=0, til...  33.3 us
    gather x1, local copies, waits for them, and re-layouts, move_rows(): return (arrived[placed], arrived_labels[placed, 1])  25.9 us
    gather x1, local copies, waits for them, and re-layouts, move_rows(): rows[ordering]  25.1 us
    dot_general x1, matrix products, finish_rows(): jnp.dot(inner_act, perceptron_exit_map, preferred_element_type=jnp.float32)  15.5 us
  transfers between devices with their start and end apart: 3, of which 1 were waited for; matrix products, arithmetic and copies ran while one was open for 59% of the time, Pallas kernels for 0%

profile of v1, /device:TPU:1, one launch (start us, length us, event | category | flops | bytes accessed | tf_op | source)
XLA Modules:
  0.0 407.6 jit_solution(14218376634625026899)
XLA Ops:
  0.0 0.0 copy-start
  0.0 0.0 copy-start.12
  0.0 1.3 broadcast_in_dim.8
  1.3 6.9 %all-to-all-start = ((f32[8,1,2]{2,1,0:T(1,128)}), f32[8,1,2]{2,1,0:T(1,128)S(1)}, u32[]{:S(2)}, u32[]{:S(2)}) async-start(f32[8,1,2]{2,1,0:T(1,128)} %broadcast_in_dim.8), calls=%async_computation | async-start | bytes 8192 | tf_op jit(solution)/shard_map/all_to_all | solution.py:17
  8.2 4.6 %copy.45 = bf16[6144,256]{0,1:T(8,128)(2,1)} copy(bf16[6144,256]{1,0:T(8,128)(2,1)} %param.20) | data formatting | bytes 6291456 | tf_op args[0]
  12.8 2.6 convert_reduce_fusion
  15.4 2.7 fusion.27
  18.2 0.0 copy-start.2
  18.2 5.3 %convolution_convert_fusion.2 = bf16[6144,256]{0,1:T(8,128)(2,1)} fusion(bf16[256,256]{1,0:T(8,128)(2,1)S(1)} %copy-done.12, bf16[6144,256]{0,1:T(8,128)(2,1)} %copy.45, f32[256]{0:T(256)S(1)} %copy-done.19, f32[256]{0:T(256)S(1)} %copy-done.20, f32[6144]{0:T(1024)S(1)} %add_rsqrt_fusion.1, f32[6144]{0:T(1024)S(1)} %broadcast_multiply_fusion.1), kind=kOutput, calls=%fused_computation.36 | convolution fusion | flops 816316416 | bytes 6473728 | tf_op jit(solution)/shard_map/dot_general | solution.py:151
  23.5 3.4 convolution_convert_fusion.1
  27.0 6.7 %sort.34 = (s32[6144]{0:T(1024)}, s32[6144]{0:T(1024)S(1)}) sort(s32[6144]{0:T(1024)S(1)} %fusion.46, s32[6144]{0:T(1024)S(1)} %iota.11), dimensions={0}, to_apply=%region_19.20 | sort | flops 79872 | bytes 98304 | tf_op jit(solution)/shard_map/jit(argsort)/sort | solution.py:135
  33.7 0.0 copy-start.7
  33.7 34.3 %gather_fusion.1 = s32[6144]{0:T(1024)S(1)} fusion(s32[6144]{0:T(1024)S(1)} %copy-done.2, s32[6144]{0:T(1024)S(1)} %get-tuple-element.17), kind=kCustom, calls=%fused_computation.1 | custom fusion | bytes 73728 | tf_op jit(solution)/shard_map/gather | solution.py:137
  68.1 0.0 copy-start.17
  68.1 0.0 copy-start.24
  68.1 34.3 %gather_fusion.2 = s32[6144]{0:T(1024)S(1)} fusion(s32[6144]{0:T(1024)S(1)} %get-tuple-element.18, s32[6144]{0:T(1024)S(1)} %get-tuple-element.17), kind=kCustom, calls=%fused_computation.2 | custom fusion | bytes 73728 | tf_op jit(solution)/shard_map/gather | solution.py:137
  102.4 0.1 stack.10
  102.5 0.1 stack.9
  102.6 0.8 copy.52
  103.3 0.0 all-to-all-done
  103.3 11.3 %all-to-all-start.2 = ((s32[128,48,2]{1,2,0:T(2,128)}), s32[128,48,2]{1,2,0:T(2,128)}, u32[]{:S(2)}, u32[]{:S(2)}) async-start(s32[128,48,2]{1,2,0:T(2,128)} %copy.52), calls=%async_computation.2 | async-start | bytes 262144 | tf_op jit(solution)/shard_map/all_to_all | solution.py:46
  114.6 0.5 broadcast.106
  115.1 0.6 reduce.3
  115.8 0.1 div.64
  115.9 10.9 %fusion.93 = (f32[6144,16]{0,1:T(8,128)S(1)}, f32[6144,16,32]{0,2,1:T(8,128)}) fusion(bf16[6144,16,16]{0,2,1:T(8,128)(2,1)} %bitcast.68, f32[16]{0:T(128)S(1)} %div.64, f32[32]{0:T(128)S(1)} %copy-done.24, bf16[16,32]{1,0:T(8,128)(2,1)S(1)} %copy-done.17), kind=kOutput, calls=%fused_computation.125 | convolution fusion | flops 113246240 | bytes 16123072 | tf_op jit(solution)/shard_map/sub | solution.py:161
  126.8 9.1 %fusion.31 = (f32[16,32]{1,0:T(8,128)S(1)}, bf16[6144,16,32]{0,2,1:T(8,128)(2,1)}) fusion(f32[6144,16,32]{0,2,1:T(8,128)} %get-tuple-element.12, f32[6144,16]{0,1:T(8,128)S(1)} %get-tuple-element.11), kind=kLoop, calls=%fused_computation.47 | loop fusion | flops 9436672 | bytes 19269632 | tf_op jit(solution)/shard_map/reduce_sum | solution.py:163
  135.8 0.0 copy-start.10
  135.8 4.6 %fusion.98 = f32[16,32,16]{1,2,0:T(8,128)S(1)} fusion(bf16[6144,16,32]{0,2,1:T(8,128)(2,1)} %get-tuple-element.10, bf16[6144,16,16]{0,2,1:T(8,128)(2,1)S(1)} %bitcast.56), kind=kOutput, calls=%fused_computation.128 | convolution fusion | flops 100663296 | bytes 9469952 | tf_op jit(solution)/shard_map/qct,qcv->ctv/dot_general | solution.py:164
  140.4 12.0 %all-gather = f32[64,32,16]{1,2,0:T(8,128)S(1)} all-gather(f32[16,32,16]{1,2,0:T(8,128)S(1)} %fusion.98), channel_id=2, replica_groups=mesh['head_0'=4,'head_1'=2,'pts_0'=2,'pts_1'=4,'pts_2'=2] {'head_0'}, dimensions={0}, use_global_device_ids=true | all-gather | bytes 163840 | tf_op jit(solution)/shard_map/all_gather | solution.py:33
  152.4 4.5 %all-gather.1 = f32[32,32,16]{1,2,0:T(8,128)S(1)} all-gather(f32[16,32,16]{1,2,0:T(8,128)S(1)} %reduce_sum.156), channel_id=3, replica_groups=mesh['head_0'=4,'head_1'=2,'pts_0'=2,'pts_1'=4,'pts_2'=2] {'head_1'}, dimensions={0}, use_global_device_ids=true | all-gather | bytes 98304 | tf_op jit(solution)/shard_map/all_gather | solution.py:33
  156.9 6.2 %all-gather.2 = f32[32,32,16]{1,2,0:T(8,128)S(1)} all-gather(f32[16,32,16]{1,2,0:T(8,128)S(1)} %reduce_sum.157), channel_id=4, replica_groups=mesh['head_0'=4,'head_1'=2,'pts_0'=2,'pts_1'=4,'pts_2'=2] {'pts_0'}, dimensions={0}, use_global_device_ids=true | all-gather | bytes 98304 | tf_op jit(solution)/shard_map/all_gather | solution.py:33
  163.2 10.6 %all-gather.3 = f32[64,32,16]{1,2,0:T(8,128)S(1)} all-gather(f32[16,32,16]{1,2,0:T(8,128)S(1)} %reduce_sum.158), channel_id=5, replica_groups=mesh['head_0'=4,'head_1'=2,'pts_0'=2,'pts_1'=4,'pts_2'=2] {'pts_1'}, dimensions={0}, use_global_device_ids=true | all-gather | bytes 163840 | tf_op jit(solution)/shard_map/all_gather | solution.py:33
  173.8 8.7 %all-gather.4 = f32[32,32,16]{1,2,0:T(8,128)S(1)} all-gather(f32[16,32,16]{1,2,0:T(8,128)S(1)} %reduce_sum.159), channel_id=6, replica_groups=mesh['head_0'=4,'head_1'=2,'pts_0'=2,'pts_1'=4,'pts_2'=2] {'pts_2'}, dimensions={0}, use_global_device_ids=true | all-gather | bytes 98304 | tf_op jit(solution)/shard_map/all_gather | solution.py:33
  182.5 9.4 %all-gather.5 = f32[64,32]{1,0:T(8,128)S(1)} all-gather(f32[16,32]{1,0:T(8,128)S(1)} %get-tuple-element.9), channel_id=7, replica_groups=mesh['head_0'=4,'head_1'=2,'pts_0'=2,'pts_1'=4,'pts_2'=2] {'head_0'}, dimensions={0}, use_global_device_ids=true | all-gather | bytes 10240 | tf_op jit(solution)/shard_map/all_gather | solution.py:33
  191.9 3.2 all-gather.6
  195.1 5.0 %all-gather.7 = f32[32,32]{1,0:T(8,128)S(1)} all-gather(f32[16,32]{1,0:T(8,128)S(1)} %reduce_sum.163), channel_id=9, replica_groups=mesh['head_0'=4,'head_1'=2,'pts_0'=2,'pts_1'=4,'pts_2'=2] {'pts_0'}, dimensions={0}, use_global_device_ids=true | all-gather | bytes 6144 | tf_op jit(solution)/shard_map/all_gather | solution.py:33
  200.1 9.2 %all-gather.8 = f32[64,32]{1,0:T(8,128)S(1)} all-gather(f32[16,32]{1,0:T(8,128)S(1)} %reduce_sum.164), channel_id=10, replica_groups=mesh['head_0'=4,'head_1'=2,'pts_0'=2,'pts_1'=4,'pts_2'=2] {'pts_1'}, dimensions={0}, use_global_device_ids=true | all-gather | bytes 10240 | tf_op jit(solution)/shard_map/all_gather | solution.py:33
  209.3 9.1 %all-gather.9 = f32[32,32]{1,0:T(8,128)S(1)} all-gather(f32[16,32]{1,0:T(8,128)S(1)} %reduce_sum.165), channel_id=11, replica_groups=mesh['head_0'=4,'head_1'=2,'pts_0'=2,'pts_1'=4,'pts_2'=2] {'pts_2'}, dimensions={0}, use_global_device_ids=true | all-gather | bytes 6144 | tf_op jit(solution)/shard_map/all_gather | solution.py:33
  218.5 0.3 fusion.56
  218.8 0.3 fusion.58
  219.1 0.3 fusion.54
  219.4 0.6 fusion.94
  220.1 0.1 fusion.42
  220.1 0.4 convolution_convert_fusion.3
  220.5 3.8 convolution_convert_fusion
  224.3 0.0 copy-start.18
  224.3 0.0 copy-start.21
  224.3 0.0 copy-start.22
  224.4 1.4 fusion.95
  225.8 0.7 multiply_reduce_fusion
  226.5 1.9 copy-done.5
  228.4 0.0 copy-start.11
  228.4 0.0 copy-start.23
  228.4 58.5 %fusion.119 = bf16[6144,1024]{1,0:T(8,128)(2,1)} fusion(f32[1024]{0:T(1024)S(1)} %copy-done.18, bf16[256,1024]{1,0:T(8,128)(2,1)S(1)} %copy-done, f32[6144,256]{0,1:T(8,128)S(1)} %get-tuple-element.16, f32[256]{0:T(256)S(1)} %copy-done.21, f32[256]{0:T(256)S(1)} %copy-done.22, f32[6144]{0:T(1024)S(1)} %add_rsqrt_fusion, ...), kind=kOutput, calls=%fused_computation.8.clone.clone.clone.clone.clone.clone.clone.clone.1 | convolution fusion | flops 3644325888 | bytes 19453952 | tf_op jit(solution)/shard_map/dot_general | solution.py:96
  286.9 15.5 %fusion.22 = bf16[6144,256]{0,1:T(8,128)(2,1)} fusion(f32[6144,256]{0,1:T(8,128)} %copy-done.5, bf16[1024,256]{1,0:T(8,128)(2,1)S(1)} %copy-done.11, f32[256]{0:T(256)S(1)} %copy-done.23, bf16[6144,1024]{1,0:T(8,128)(2,1)} %fusion.119), kind=kOutput, calls=%fused_computation.37 | convolution fusion | flops 3225944064 | bytes 22545408 | tf_op jit(solution)/shard_map/dot_general | solution.py:102
  302.4 3.2 copy.51
  305.6 25.1 %gather_fusion = bf16[6144,256]{1,0:T(8,128)(2,1)} fusion(bf16[6144,256]{1,0:T(8,128)(2,1)S(1)} %copy.51, s32[6144]{0:T(1024)S(1)} %copy-done.8), kind=kCustom, calls=%fused_computation | custom fusion | bytes 6316032 | tf_op jit(solution)/shard_map/gather | solution.py:45
  330.7 0.0 all-to-all-done.2
  330.7 9.6 %all-to-all-start.1 = ((bf16[128,48,256]{2,1,0:T(8,128)(2,1)}), bf16[128,48,256]{2,1,0:T(8,128)(2,1)}, u32[]{:S(2)}, u32[]{:S(2)}) async-start(bf16[128,48,256]{2,1,0:T(8,128)(2,1)} %bitcast.55), calls=%async_computation.1 | async-start | bytes 6291456 | tf_op jit(solution)/shard_map/all_to_all | solution.py:45
  340.3 0.9 copy.53
  341.2 0.1 all_to_all.23
  341.4 6.7 %sort.35 = (s32[6144]{0:T(1024)}, s32[6144]{0:T(1024)S(1)}) sort(s32[6144]{0:T(1024)S(1)} %bitcast.64, s32[6144]{0:T(1024)S(1)} %iota.13), dimensions={0}, to_apply=%region_20.21 | sort | flops 79872 | bytes 98304 | tf_op jit(solution)/shard_map/jit(argsort)/sort | solution.py:47
  348.1 33.3 %all-to-all-done.1 = bf16[128,48,256]{2,1,0:T(8,128)(2,1)} async-done(((bf16[128,48,256]{2,1,0:T(8,128)(2,1)}), bf16[128,48,256]{2,1,0:T(8,128)(2,1)}, u32[]{:S(2)}, u32[]{:S(2)}) %all-to-all-start.1) | async-done | bytes 3145760 | tf_op jit(solution)/shard_map/all_to_all | solution.py:45
  381.4 25.9 %gather_fusion.3 = bf16[6144,256]{1,0:T(8,128)(2,1)} fusion(bf16[6144,256]{1,0:T(8,128)(2,1)} %bitcast.19, s32[6144]{0:T(1024)S(1)} %fusion.48), kind=kCustom, calls=%fused_computation.3 | custom fusion | bytes 6316032 | tf_op jit(solution)/shard_map/gather | solution.py:48
  (59 shorter events, 0.4 us)
Async XLA Ops:
  0.0 228.4 %copy-start = (bf16[256,1024]{1,0:T(8,128)(2,1)S(1)}, bf16[256,1024]{1,0:T(8,128)(2,1)}, u32[]{:S(2)}) copy-start(bf16[256,1024]{1,0:T(8,128)(2,1)} %param.36) | copy-start | bytes 1572868
  0.0 18.2 %copy-start.20 = (f32[256]{0:T(256)S(1)}, f32[256]{0:T(256)}, u32[]{:S(2)}) copy-start(f32[256]{0:T(256)} %param.22) | copy-start | bytes 3076
  0.0 18.2 %copy-start.19 = (f32[256]{0:T(256)S(1)}, f32[256]{0:T(256)}, u32[]{:S(2)}) copy-start(f32[256]{0:T(256)} %param.23) | copy-start | bytes 3076
  0.0 18.2 %copy-start.12 = (bf16[256,256]{1,0:T(8,128)(2,1)S(1)}, bf16[256,256]{1,0:T(8,128)(2,1)}, u32[]{:S(2)}) copy-start(bf16[256,256]{1,0:T(8,128)(2,1)} %param.25) | copy-start | bytes 393220
  1.3 102.0 %all-to-all-start = ((f32[8,1,2]{2,1,0:T(1,128)}), f32[8,1,2]{2,1,0:T(1,128)S(1)}, u32[]{:S(2)}, u32[]{:S(2)}) async-start(f32[8,1,2]{2,1,0:T(1,128)} %broadcast_in_dim.8), calls=%async_computation | async-start | bytes 8192 | tf_op jit(solution)/shard_map/all_to_all | solution.py:17
  12.8 10.7 %copy-start.3 = (bf16[6144,256]{0,1:T(8,128)(2,1)S(1)}, bf16[6144,256]{0,1:T(8,128)(2,1)}, u32[]{:S(2)}) copy-start(bf16[6144,256]{0,1:T(8,128)(2,1)} %copy.45) | copy-start | bytes 9437188
  12.8 10.7 %copy-start.13 = (bf16[256,256]{1,0:T(8,128)(2,1)S(1)}, bf16[256,256]{1,0:T(8,128)(2,1)}, u32[]{:S(2)}) copy-start(bf16[256,256]{1,0:T(8,128)(2,1)} %param.24) | copy-start | bytes 393220
  18.2 8.7 %copy-start.2 = (s32[6144]{0:T(1024)S(1)}, s32[6144]{0:T(1024)}, u32[]{:S(2)}) copy-start(s32[6144]{0:T(1024)} %param.21) | copy-start | bytes 73732
  33.7 34.3 %copy-start.7 = (s32[6144]{0:T(1024)}, s32[6144]{0:T(1024)S(1)}, u32[]{:S(2)}) copy-start(s32[6144]{0:T(1024)S(1)} %get-tuple-element.17) | copy-start | bytes 73732
  68.1 47.8 %copy-start.17 = (bf16[16,32]{1,0:T(8,128)(2,1)S(1)}, bf16[16,32]{1,0:T(8,128)(2,1)}, u32[]{:S(2)}) copy-start(bf16[16,32]{1,0:T(8,128)(2,1)} %param.26) | copy-start | bytes 3076
  68.1 47.8 %copy-start.24 = (f32[32]{0:T(128)S(1)}, f32[32]{0:T(128)}, u32[]{:S(2)}) copy-start(f32[32]{0:T(128)} %param.27) | copy-start | bytes 388
  103.3 227.4 %all-to-all-start.2 = ((s32[128,48,2]{1,2,0:T(2,128)}), s32[128,48,2]{1,2,0:T(2,128)}, u32[]{:S(2)}, u32[]{:S(2)}) async-start(s32[128,48,2]{1,2,0:T(2,128)} %copy.52), calls=%async_computation.2 | async-start | bytes 262144 | tf_op jit(solution)/shard_map/all_to_all | solution.py:46
  126.8 9.1 %copy-start.6 = (bf16[6144,256]{0,1:T(8,128)(2,1)S(1)}, bf16[6144,256]{0,1:T(8,128)(2,1)}, u32[]{:S(2)}) copy-start(bf16[6144,256]{0,1:T(8,128)(2,1)} %convolution_convert_fusion.1) | copy-start | bytes 9437188
  126.8 91.7 %copy-start.14 = (f32[16,16]{1,0:T(8,128)S(1)}, f32[16,16]{1,0:T(8,128)}, u32[]{:S(2)}) copy-start(f32[16,16]{1,0:T(8,128)} %param.30) | copy-start | bytes 3076
  126.8 92.0 %copy-start.15 = (f32[16,16]{1,0:T(8,128)S(1)}, f32[16,16]{1,0:T(8,128)}, u32[]{:S(2)}) copy-start(f32[16,16]{1,0:T(8,128)} %param.29) | copy-start | bytes 3076
  135.8 83.3 %copy-start.16 = (f32[16,16]{1,0:T(8,128)S(1)}, f32[16,16]{1,0:T(8,128)}, u32[]{:S(2)}) copy-start(f32[16,16]{1,0:T(8,128)} %param.31) | copy-start | bytes 3076
  135.8 88.5 %copy-start.9 = (bf16[256,256]{1,0:T(8,128)(2,1)S(1)}, bf16[256,256]{1,0:T(8,128)(2,1)}, u32[]{:S(2)}) copy-start(bf16[256,256]{1,0:T(8,128)(2,1)} %param.32) | copy-start | bytes 393220
  135.8 88.5 %copy-start.10 = (f32[256]{0:T(256)S(1)}, f32[256]{0:T(256)}, u32[]{:S(2)}) copy-start(f32[256]{0:T(256)} %param.33) | copy-start | bytes 3076
  218.4 5.9 %copy-start.4 = (bf16[6144,256]{0,1:T(8,128)(2,1)S(1)}, bf16[6144,256]{0,1:T(8,128)(2,1)}, u32[]{:S(2)}) copy-start(bf16[6144,256]{0,1:T(8,128)(2,1)} %copy.45) | copy-start | bytes 9437188
  224.3 4.1 %copy-start.18 = (f32[1024]{0:T(1024)S(1)}, f32[1024]{0:T(1024)}, u32[]{:S(2)}) copy-start(f32[1024]{0:T(1024)} %param.37) | copy-start | bytes 12292
  224.3 4.1 %copy-start.21 = (f32[256]{0:T(256)S(1)}, f32[256]{0:T(256)}, u32[]{:S(2)}) copy-start(f32[256]{0:T(256)} %param.35) | copy-start | bytes 3076
  224.3 4.1 %copy-start.22 = (f32[256]{0:T(256)S(1)}, f32[256]{0:T(256)}, u32[]{:S(2)}) copy-start(f32[256]{0:T(256)} %param.34) | copy-start | bytes 3076
  225.8 2.6 copy-start.5
  228.4 58.5 %copy-start.11 = (bf16[1024,256]{1,0:T(8,128)(2,1)S(1)}, bf16[1024,256]{1,0:T(8,128)(2,1)}, u32[]{:S(2)}) copy-start(bf16[1024,256]{1,0:T(8,128)(2,1)} %param.38) | copy-start | bytes 1572868
  228.4 58.5 %copy-start.23 = (f32[256]{0:T(256)S(1)}, f32[256]{0:T(256)}, u32[]{:S(2)}) copy-start(f32[256]{0:T(256)} %param.39) | copy-start | bytes 3076
  286.9 18.7 %copy-start.8 = (s32[6144]{0:T(1024)S(1)}, s32[6144]{0:T(1024)}, u32[]{:S(2)}) copy-start(s32[6144]{0:T(1024)} %copy-done.7) | copy-start | bytes 73732
  330.7 50.7 %all-to-all-start.1 = ((bf16[128,48,256]{2,1,0:T(8,128)(2,1)}), bf16[128,48,256]{2,1,0:T(8,128)(2,1)}, u32[]{:S(2)}, u32[]{:S(2)}) async-start(bf16[128,48,256]{2,1,0:T(8,128)(2,1)} %bitcast.55), calls=%async_computation.1 | async-start | bytes 6291456 | tf_op jit(solution)/shard_map/all_to_all | solution.py:45
  381.4 25.9 %copy-start.1 = (bf16[256,1024]{1,0:T(8,128)(2,1)S(1)}, bf16[256,1024]{1,0:T(8,128)(2,1)}, u32[]{:S(2)}) copy-start(bf16[256,1024]{1,0:T(8,128)(2,1)} %param.36) | copy-start | bytes 1572868
